TPU v7x, 32 devices: a whole 2x2x4 slice. The times are simulated.
32 devices in a mesh: grp: 4 (over y, x), row: 8 (over z, core).
Axes of the slice: x: 2, y: 2, z: 4, core: 2. Of those that a mesh axis runs over, the one named last changes fastest.
Arguments:
- tiles: bfloat16 [4, 8, 32, 256, 256], P('grp', 'row'), may hold values from -0.046875 to 0.046875
- tile_rows: int32 [4, 8, 32], P('grp', 'row'), may hold values from 0 to 3, as said below
- tile_cols: int32 [4, 8, 32], P('grp', 'row'), may hold values from 0 to 7, as said below
- live_tiles: int32 [4, 8], P('grp', 'row'), may hold values from 16 to 32, as said below
- dual_shift: float32 [8192], P('row'), may hold values from 0.5 to 2
- start_block: float32 [32, 8192], P(None, 'row'), may hold values from -6 to 6
Outputs:
- projections: float32 [4, 32, 128], replicated
- factors: float32 [4, 32, 32], replicated
- next_block: float32 [32, 8192], P(None, 'row')
Inputs may be any that keep to these rules, and one draw needn't show every extreme that they name: `tile_rows`: the tile slots of one device sit at distinct positions (block row, column block), padding slots included. `tile_cols`: column block j of group g is global block column (j // 1) * 4 + g * 1 + j % 1. Slots from live_tiles on are padding with arbitrary values; in every draw some device has all 32 slots live.
All inputs are finite; a program needn't handle non-finite values.
Results may differ from a plain program's by a relative error of at most 0.013.
Values may be sent and summed in bfloat16 or wider, within the bound.
A program may use at most 64 MiB of HBM per device.

v0:
```python
import jax
import jax.numpy as jnp
from jax import lax
from jax.sharding import PartitionSpec as P

ITERS = 4


def inner_product(left, right):
    return lax.dot_general(
        left,
        right,
        (((1,), (1,)), ((), ())),
        precision=lax.Precision.HIGHEST,
        preferred_element_type=jnp.float32,
    )


def apply_matrix(left, right):
    return jnp.dot(left, right, precision=lax.Precision.HIGHEST, preferred_element_type=jnp.float32)


def per_device(tiles, tile_rows, tile_cols, live_tiles, dual_shift, start_block):
    matrix = tiles[0, 0]
    rows_here = tile_rows[0, 0]
    cols_here = tile_cols[0, 0]
    tile_count = matrix.shape[0]
    tile_edge = matrix.shape[1]
    vec_width = start_block.shape[0]
    row_count = start_block.shape[1]
    group_count = lax.axis_size("grp")
    owner_count = lax.axis_size("row")
    owned_blocks = row_count // tile_edge
    quarter_tiles = owned_blocks // group_count
    column_tiles = quarter_tiles * owner_count
    group_index = lax.axis_index("grp")
    live_mask = (jnp.arange(tile_count) < live_tiles[0, 0]).astype(jnp.float32)
    row_table = (rows_here[:, None] == jnp.arange(owned_blocks)[None, :]).astype(
        jnp.float32
    ) * live_mask[:, None]
    col_table = (cols_here[:, None] == jnp.arange(column_tiles)[None, :]).astype(
        jnp.float32
    ) * live_mask[:, None]

    def partial_of(full_rows, group_rows):
        gathered = lax.all_gather(group_rows, "row", axis=1, tiled=True)
        forward = jnp.einsum(
            "kbc,brc->kbr",
            jnp.take(gathered, cols_here, axis=1),
            matrix,
            preferred_element_type=jnp.float32,
        )
        direct = jnp.einsum("kbr,bi->kir", forward, row_table)
        backward = jnp.einsum(
            "kbr,brc->kbc",
            jnp.take(full_rows, rows_here, axis=1),
            matrix,
            preferred_element_type=jnp.float32,
        )
        spread = jnp.einsum("kbc,bj->kjc", backward, col_table)
        mine = lax.psum_scatter(spread, "row", scatter_dimension=1, tiled=True)
        placed = lax.dynamic_update_slice_in_dim(
            jnp.zeros_like(direct), mine, group_index * quarter_tiles, 1
        )
        return 0.5 * (direct + placed)

    def split_parts(vectors):
        rounded = vectors.astype(jnp.bfloat16).reshape(vec_width, owned_blocks, tile_edge)
        return (
            rounded,
            lax.dynamic_slice_in_dim(rounded, group_index * quarter_tiles, quarter_tiles, 1),
        )

    def finish_sum(partial_value):
        return lax.psum(partial_value, "grp").reshape(vec_width, row_count)

    def reduce_dots(values):
        return lax.psum(values, "row")

    def orthonormal(block, gram_matrix):
        lower_factor = jnp.linalg.cholesky(gram_matrix)
        return (
            lax.linalg.triangular_solve(lower_factor, block, left_side=True, lower=True),
            lower_factor,
        )

    current, unused = orthonormal(start_block, reduce_dots(inner_product(start_block, start_block)))
    total_cols = ITERS * vec_width
    basis_rows = jnp.zeros((total_cols, current.shape[1]), jnp.float32)
    projections = jnp.zeros((ITERS, vec_width, total_cols), jnp.float32)
    factors = jnp.zeros((ITERS, vec_width, vec_width), jnp.float32)

    def lanczos_step(step_index, state_now):
        current, basis_rows, projections, factors = state_now
        basis_rows = lax.dynamic_update_slice_in_dim(basis_rows, current, step_index * vec_width, 0)
        full_rows, group_rows = split_parts(current)
        image = finish_sum(partial_of(full_rows, group_rows)) - current * dual_shift[None, :]
        first_coef, square_sum = reduce_dots(
            (inner_product(image, basis_rows), inner_product(image, image))
        )
        image = image - apply_matrix(first_coef, basis_rows)
        gram_matrix = square_sum - inner_product(first_coef, first_coef)
        current, lower_factor = orthonormal(image, gram_matrix)
        projections = lax.dynamic_update_index_in_dim(projections, first_coef, step_index, 0)
        factors = lax.dynamic_update_index_in_dim(factors, lower_factor, step_index, 0)
        return (current, basis_rows, projections, factors)

    current, basis_rows, projections, factors = lax.fori_loop(
        0, ITERS, lanczos_step, (current, basis_rows, projections, factors)
    )
    return (projections, factors, current)


def solution(mesh):
    in_specs = (
        P("grp", "row", None, None, None),
        P("grp", "row", None),
        P("grp", "row", None),
        P("grp", "row"),
        P("row"),
        P(None, "row"),
    )
    out_specs = (P(), P(), P(None, "row"))
    return jax.shard_map(
        per_device, mesh=mesh, in_specs=in_specs, out_specs=out_specs, check_vma=False
    )
```

profile of v0, /device:TPU:0, one launch (start us, length us, event | category | flops | bytes accessed | tf_op | source)
XLA Modules:
  0.0 526.2 jit_solution(8943379851777965999)
XLA Ops:
  8.3 30.3 %psum.46 = f32[32,32]{0,1:T(8,128)S(1)} all-reduce(f32[32,32]{0,1:T(8,128)S(1)} %fusion.41), channel_id=1, replica_groups=mesh['grp'=4,'row'=8] {'row'}, use_global_device_ids=true, to_apply=%region_0.0 | all-reduce | flops 1024 | bytes 8192 | tf_op jit(solution)/shard_map/psum | solution.py:78
  46.5 472.2 %while.23 = (s32[]{:T(128)}, f32[32,1024]{1,0:T(8,128)S(1)}, f32[128,1024]{1,0:T(8,128)S(1)}, f32[4,32,128]{2,1,0:T(8,128)}, f32[4,32,32]{2,1,0:T(8,128)}, /*ind...) while((s32[]{:T(128)}, f32[32,1024]{1,0:T(8,128)S(1)}, ...), condition=%wide.region_8.11_spmd.clone.clone, body=%wide.region_3.10_spmd.clone.clone.sunk | while | flops 402879840 | bytes 20164480 | solution.py:108
  48.5 3.0 convolution_bitcast_fusion.7
  52.9 14.0 %all_gather.12 = bf16[32,8,256]{2,0,1:T(8,128)(2,1)S(1)} all-gather(bf16[32,1,256]{2,0,1:T(8,128)(2,1)S(1)} %copy.62), channel_id=1, replica_groups=mesh['grp'=4,'row'=8] {'row'}, dimensions={1}, use_global_device_ids=true | all-gather | bytes 147456 | tf_op jit(solution)/shard_map/while/body/eval_jaxpr/all_gather | solution.py:46
  67.5 3.5 convolution_bitcast_fusion.6
  71.5 10.4 %reduce-scatter.2.cloned.1.call-done = f32[32,1,256]{2,0,1:T(8,128)} async-done(((f32[32,8,256]{2,0,1:T(8,128)}), f32[32,1,256]{2,0,1:T(8,128)}) %reduce-scatter.2.cloned.1.call-update) | async-done | bytes 32784 | tf_op jit(solution)/shard_map/while/body/eval_jaxpr/reduce_scatter | solution.py:61
  83.6 42.2 %all-reduce.5.cloned.1.call-done = f32[32,1024]{1,0:T(8,128)} async-done(((f32[32,1024]{1,0:T(8,128)}), f32[32,1024]{1,0:T(8,128)}) %all-reduce.5.cloned.1.call-update) | async-done | bytes 131088 | tf_op jit(solution)/shard_map/while/body/eval_jaxpr/psum | solution.py:75
  127.7 28.1 %all-reduce.2 = (f32[32,128]{1,0:T(8,128)S(1)}, f32[32,32]{0,1:T(8,128)S(1)}) all-reduce(f32[32,128]{1,0:T(8,128)S(1)} %fusion.102, f32[32,32]{0,1:T(8,128)S(1)} %fusion.103), channel_id=1, replica_groups=mesh['grp'=4,'row'=8] {'row'}, use_global_device_ids=true, to_apply=%region_7.9 | all-reduce | flops 5120 | bytes 40960 | tf_op jit(solution)/shard_map/while/body/eval_jaxpr/psum | solution.py:78
  167.4 3.0 convolution_bitcast_fusion.7
  171.8 14.0 %all_gather.12 = bf16[32,8,256]{2,0,1:T(8,128)(2,1)S(1)} all-gather(bf16[32,1,256]{2,0,1:T(8,128)(2,1)S(1)} %copy.62), channel_id=1, replica_groups=mesh['grp'=4,'row'=8] {'row'}, dimensions={1}, use_global_device_ids=true | all-gather | bytes 147456 | tf_op jit(solution)/shard_map/while/body/eval_jaxpr/all_gather | solution.py:46
  186.4 3.5 convolution_bitcast_fusion.6
  190.4 9.6 %reduce-scatter.2.cloned.1.call-done = f32[32,1,256]{2,0,1:T(8,128)} async-done(((f32[32,8,256]{2,0,1:T(8,128)}), f32[32,1,256]{2,0,1:T(8,128)}) %reduce-scatter.2.cloned.1.call-update) | async-done | bytes 32784 | tf_op jit(solution)/shard_map/while/body/eval_jaxpr/reduce_scatter | solution.py:61
  201.7 41.9 %all-reduce.5.cloned.1.call-done = f32[32,1024]{1,0:T(8,128)} async-done(((f32[32,1024]{1,0:T(8,128)}), f32[32,1024]{1,0:T(8,128)}) %all-reduce.5.cloned.1.call-update) | async-done | bytes 131088 | tf_op jit(solution)/shard_map/while/body/eval_jaxpr/psum | solution.py:75
  245.4 28.1 %all-reduce.2 = (f32[32,128]{1,0:T(8,128)S(1)}, f32[32,32]{0,1:T(8,128)S(1)}) all-reduce(f32[32,128]{1,0:T(8,128)S(1)} %fusion.102, f32[32,32]{0,1:T(8,128)S(1)} %fusion.103), channel_id=1, replica_groups=mesh['grp'=4,'row'=8] {'row'}, use_global_device_ids=true, to_apply=%region_7.9 | all-reduce | flops 5120 | bytes 40960 | tf_op jit(solution)/shard_map/while/body/eval_jaxpr/psum | solution.py:78
  289.5 14.0 %all_gather.12 = bf16[32,8,256]{2,0,1:T(8,128)(2,1)S(1)} all-gather(bf16[32,1,256]{2,0,1:T(8,128)(2,1)S(1)} %copy.62), channel_id=1, replica_groups=mesh['grp'=4,'row'=8] {'row'}, dimensions={1}, use_global_device_ids=true | all-gather | bytes 147456 | tf_op jit(solution)/shard_map/while/body/eval_jaxpr/all_gather | solution.py:46
  304.1 3.5 convolution_bitcast_fusion.6
  308.1 9.6 %reduce-scatter.2.cloned.1.call-done = f32[32,1,256]{2,0,1:T(8,128)} async-done(((f32[32,8,256]{2,0,1:T(8,128)}), f32[32,1,256]{2,0,1:T(8,128)}) %reduce-scatter.2.cloned.1.call-update) | async-done | bytes 32784 | tf_op jit(solution)/shard_map/while/body/eval_jaxpr/reduce_scatter | solution.py:61
  319.5 41.9 %all-reduce.5.cloned.1.call-done = f32[32,1024]{1,0:T(8,128)} async-done(((f32[32,1024]{1,0:T(8,128)}), f32[32,1024]{1,0:T(8,128)}) %all-reduce.5.cloned.1.call-update) | async-done | bytes 131088 | tf_op jit(solution)/shard_map/while/body/eval_jaxpr/psum | solution.py:75
  363.1 28.1 %all-reduce.2 = (f32[32,128]{1,0:T(8,128)S(1)}, f32[32,32]{0,1:T(8,128)S(1)}) all-reduce(f32[32,128]{1,0:T(8,128)S(1)} %fusion.102, f32[32,32]{0,1:T(8,128)S(1)} %fusion.103), channel_id=1, replica_groups=mesh['grp'=4,'row'=8] {'row'}, use_global_device_ids=true, to_apply=%region_7.9 | all-reduce | flops 5120 | bytes 40960 | tf_op jit(solution)/shard_map/while/body/eval_jaxpr/psum | solution.py:78
  407.3 14.0 %all_gather.12 = bf16[32,8,256]{2,0,1:T(8,128)(2,1)S(1)} all-gather(bf16[32,1,256]{2,0,1:T(8,128)(2,1)S(1)} %copy.62), channel_id=1, replica_groups=mesh['grp'=4,'row'=8] {'row'}, dimensions={1}, use_global_device_ids=true | all-gather | bytes 147456 | tf_op jit(solution)/shard_map/while/body/eval_jaxpr/all_gather | solution.py:46
  421.8 3.5 convolution_bitcast_fusion.6
  425.8 9.7 %reduce-scatter.2.cloned.1.call-done = f32[32,1,256]{2,0,1:T(8,128)} async-done(((f32[32,8,256]{2,0,1:T(8,128)}), f32[32,1,256]{2,0,1:T(8,128)}) %reduce-scatter.2.cloned.1.call-update) | async-done | bytes 32784 | tf_op jit(solution)/shard_map/while/body/eval_jaxpr/reduce_scatter | solution.py:61
  437.2 42.0 %all-reduce.5.cloned.1.call-done = f32[32,1024]{1,0:T(8,128)} async-done(((f32[32,1024]{1,0:T(8,128)}), f32[32,1024]{1,0:T(8,128)}) %all-reduce.5.cloned.1.call-update) | async-done | bytes 131088 | tf_op jit(solution)/shard_map/while/body/eval_jaxpr/psum | solution.py:75
  481.0 28.1 %all-reduce.2 = (f32[32,128]{1,0:T(8,128)S(1)}, f32[32,32]{0,1:T(8,128)S(1)}) all-reduce(f32[32,128]{1,0:T(8,128)S(1)} %fusion.102, f32[32,32]{0,1:T(8,128)S(1)} %fusion.103), channel_id=1, replica_groups=mesh['grp'=4,'row'=8] {'row'}, use_global_device_ids=true, to_apply=%region_7.9 | all-reduce | flops 5120 | bytes 40960 | tf_op jit(solution)/shard_map/while/body/eval_jaxpr/psum | solution.py:78
  (199 shorter events, 84.2 us)
Async XLA Ops:
  7.2 0.9 copy-start
  46.5 5.1 copy-start.3
  46.5 35.4 %reduce-scatter.2.cloned.1.call-start = ((), (), s32[]{:S(2)}) async-start(), calls=%async_computation.1 | async-start | bytes 294912 | tf_op jit(solution)/shard_map/while/body/eval_jaxpr/reduce_scatter | solution.py:61
  51.5 19.5 %copy-start.4 = (s32[32]{0:T(128)S(1)}, s32[32]{0:T(128)}, u32[]{:S(2)}) copy-start(s32[32]{0:T(128)} %get-tuple-element.492) | copy-start | bytes 388 | tf_op jit(solution)/shard_map/while
  52.7 73.2 %copy-start.2 = (f32[1024]{0:T(1024)S(1)}, f32[1024]{0:T(1024)}, u32[]{:S(2)}) copy-start(f32[1024]{0:T(1024)} %get-tuple-element.493) | copy-start | bytes 12292 | tf_op jit(solution)/shard_map/while
  52.8 73.1 %all-reduce.5.cloned.1.call-start = ((), (), s32[]{:S(2)}) async-start(), calls=%async_computation.2 | async-start | bytes 262144 | tf_op jit(solution)/shard_map/while/body/eval_jaxpr/psum | solution.py:75
  165.4 5.1 copy-start.3
  165.4 34.6 %reduce-scatter.2.cloned.1.call-start = ((), (), s32[]{:S(2)}) async-start(), calls=%async_computation.1 | async-start | bytes 294912 | tf_op jit(solution)/shard_map/while/body/eval_jaxpr/reduce_scatter | solution.py:61
  170.4 19.5 %copy-start.4 = (s32[32]{0:T(128)S(1)}, s32[32]{0:T(128)}, u32[]{:S(2)}) copy-start(s32[32]{0:T(128)} %get-tuple-element.492) | copy-start | bytes 388 | tf_op jit(solution)/shard_map/while
  171.6 72.0 %copy-start.2 = (f32[1024]{0:T(1024)S(1)}, f32[1024]{0:T(1024)}, u32[]{:S(2)}) copy-start(f32[1024]{0:T(1024)} %get-tuple-element.493) | copy-start | bytes 12292 | tf_op jit(solution)/shard_map/while
  171.6 72.0 %all-reduce.5.cloned.1.call-start = ((), (), s32[]{:S(2)}) async-start(), calls=%async_computation.2 | async-start | bytes 262144 | tf_op jit(solution)/shard_map/while/body/eval_jaxpr/psum | solution.py:75
  283.1 5.1 copy-start.3
  283.1 34.6 %reduce-scatter.2.cloned.1.call-start = ((), (), s32[]{:S(2)}) async-start(), calls=%async_computation.1 | async-start | bytes 294912 | tf_op jit(solution)/shard_map/while/body/eval_jaxpr/reduce_scatter | solution.py:61
  288.1 19.5 %copy-start.4 = (s32[32]{0:T(128)S(1)}, s32[32]{0:T(128)}, u32[]{:S(2)}) copy-start(s32[32]{0:T(128)} %get-tuple-element.492) | copy-start | bytes 388 | tf_op jit(solution)/shard_map/while
  289.3 72.0 %copy-start.2 = (f32[1024]{0:T(1024)S(1)}, f32[1024]{0:T(1024)}, u32[]{:S(2)}) copy-start(f32[1024]{0:T(1024)} %get-tuple-element.493) | copy-start | bytes 12292 | tf_op jit(solution)/shard_map/while
  289.3 72.0 %all-reduce.5.cloned.1.call-start = ((), (), s32[]{:S(2)}) async-start(), calls=%async_computation.2 | async-start | bytes 262144 | tf_op jit(solution)/shard_map/while/body/eval_jaxpr/psum | solution.py:75
  400.8 5.1 copy-start.3
  400.8 34.6 %reduce-scatter.2.cloned.1.call-start = ((), (), s32[]{:S(2)}) async-start(), calls=%async_computation.1 | async-start | bytes 294912 | tf_op jit(solution)/shard_map/while/body/eval_jaxpr/reduce_scatter | solution.py:61
  405.9 19.5 %copy-start.4 = (s32[32]{0:T(128)S(1)}, s32[32]{0:T(128)}, u32[]{:S(2)}) copy-start(s32[32]{0:T(128)} %get-tuple-element.492) | copy-start | bytes 388 | tf_op jit(solution)/shard_map/while
  407.0 72.1 %copy-start.2 = (f32[1024]{0:T(1024)S(1)}, f32[1024]{0:T(1024)}, u32[]{:S(2)}) copy-start(f32[1024]{0:T(1024)} %get-tuple-element.493) | copy-start | bytes 12292 | tf_op jit(solution)/shard_map/while
  407.1 72.1 %all-reduce.5.cloned.1.call-start = ((), (), s32[]{:S(2)}) async-start(), calls=%async_computation.2 | async-start | bytes 262144 | tf_op jit(solution)/shard_map/while/body/eval_jaxpr/psum | solution.py:75
  518.7 0.7 copy-start.1
Sparse Core Ops, SparseCore 0:
  52.9 28.9 reduce-scatter.1
  85.3 40.4 all-reduce.4
  171.7 28.1 reduce-scatter.1
  203.3 40.2 all-reduce.4
  289.5 28.2 reduce-scatter.1
  321.0 40.2 all-reduce.4
  407.2 28.2 reduce-scatter.1
  438.9 40.2 all-reduce.4
where the time goes:
time: 527 us; the launch traced here: 526 us
  waiting for transfers between devices  207 us (39%)
  blocking collectives  199 us (38%)
  other arithmetic  51 us (10%)
  matrix products  36.9 us (7%)
  local copies, waits for them, and re-layouts  16 us (3%)
  between operations  14.7 us (3%)
    psum x4, waiting for transfers between devices, finish_sum(): return lax.psum(partial_value, 'grp').reshape(vec_width, row_count)  168 us
    psum x5, blocking collectives, reduce_dots(): return lax.psum(values, 'row')  143 us
    all_gather x4, blocking collectives, partial_of(): gathered = lax.all_gather(group_rows, 'row', axis=1, tiled=True)  56 us
    reduce_scatter x4, waiting for transfers between devices, partial_of(): mine = lax.psum_scatter(spread, 'row', scatter_dimension=1, tiled=True)  39.4 us
    another operation x15, other arithmetic, orthonormal(): lower_factor = jnp.linalg.cholesky(gram_matrix)  18 us
    another operation x10, other arithmetic, orthonormal(): lax.linalg.triangular_solve(lower_factor, block, left_side=True, lower=True)  15.4 us
    dot_general x4, matrix products, partial_of(): jnp.einsum('kbc,brc->kbr', jnp.take(gathered, cols_here, axis=1), matrix,...  14.2 us
    dot_general x4, matrix products, partial_of(): jnp.einsum('kbr,brc->kbc', jnp.take(full_rows, rows_here, axis=1), matrix...  12.1 us
  transfers between devices with their start and end apart: 8, of which 8 were waited for; matrix products, arithmetic and copies ran while one was open for 4% of the time, Pallas kernels for 0%

commit v1 on v0

--- a/solution.py
+++ b/solution.py
@@ -72,7 +72,7 @@
         )
 
     def finish_sum(partial_value):
-        return lax.psum(partial_value, "grp").reshape(vec_width, row_count)
+        return jnp.sum(lax.all_gather(partial_value, "grp"), axis=0).reshape(vec_width, row_count)
 
     def reduce_dots(values):
         return lax.psum(values, "row")

time: 527 us -> 386 us (0.73)
  waiting for transfers between devices: 207 us -> 39.4 us
  blocking collectives: 199 us -> 231 us
    psum x4 -> x0, waiting for transfers between devices: 168 us -> none  [finish_sum(): return lax.psum(partial_value, 'grp').reshape(vec_width, row_count)]
    all_gather x0 -> x4, blocking collectives: none -> 40.4 us  [finish_sum(): lax.all_gather(partial_value, 'grp')]
    psum x5, blocking collectives: 143 us -> 134 us  [reduce_dots(): return lax.psum(values, 'row')]
  transfers between devices with their start and end apart: 8 -> 4, of which waited for: 8 -> 4; matrix products, arithmetic and copies ran while one was open for 4% -> 5% of each run, Pallas kernels for 0% -> 0%
where the time goes in v1:
time: 386 us; the launch traced here: 385 us
  blocking collectives  231 us (60%)
  other arithmetic  48.5 us (13%)
  waiting for transfers between devices  39.4 us (10%)
  matrix products  37 us (10%)
  between operations  14.4 us (4%)
  local copies, waits for them, and re-layouts  13.4 us (3%)
    psum x5, blocking collectives, reduce_dots(): return lax.psum(values, 'row')  134 us
    all_gather x4, blocking collectives, partial_of(): gathered = lax.all_gather(group_rows, 'row', axis=1, tiled=True)  56.1 us
    all_gather x4, blocking collectives, finish_sum(): lax.all_gather(partial_value, 'grp')  40.4 us
    reduce_scatter x4, waiting for transfers between devices, partial_of(): mine = lax.psum_scatter(spread, 'row', scatter_dimension=1, tiled=True)  39.4 us
    another operation x15, other arithmetic, orthonormal(): lower_factor = jnp.linalg.cholesky(gram_matrix)  18.3 us
    another operation x10, other arithmetic, orthonormal(): lax.linalg.triangular_solve(lower_factor, block, left_side=True, lower=True)  15.6 us
    dot_general x4, matrix products, partial_of(): jnp.einsum('kbc,brc->kbr', jnp.take(gathered, cols_here, axis=1), matrix,...  14.2 us
    dot_general x4, matrix products, partial_of(): jnp.einsum('kbr,brc->kbc', jnp.take(full_rows, rows_here, axis=1), matrix...  12.2 us
  transfers between devices with their start and end apart: 4, of which 4 were waited for; matrix products, arithmetic and copies ran while one was open for 5% of the time, Pallas kernels for 0%

profile of v1, /device:TPU:0, one launch (start us, length us, event | category | flops | bytes accessed | tf_op | source)
XLA Modules:
  0.0 384.6 jit_solution(9066691512320724995)
XLA Ops:
  8.3 30.3 %psum.33 = f32[32,32]{0,1:T(8,128)S(1)} all-reduce(f32[32,32]{0,1:T(8,128)S(1)} %fusion.41), channel_id=1, replica_groups=mesh['grp'=4,'row'=8] {'row'}, use_global_device_ids=true, to_apply=%region_0.0 | all-reduce | flops 1024 | bytes 8192 | tf_op jit(solution)/shard_map/psum | solution.py:78
  46.5 331.0 %while.23 = (s32[]{:T(128)}, f32[32,1024]{1,0:T(8,128)S(1)}, f32[128,1024]{1,0:T(8,128)S(1)}, f32[4,32,128]{2,1,0:T(8,128)}, f32[4,32,32]{2,1,0:T(8,128)}, /*ind...) while((s32[]{:T(128)}, f32[32,1024]{1,0:T(8,128)S(1)}, ...), condition=%wide.region_8.11_spmd.clone.clone, body=%wide.region_3.10_spmd.clone.clone.sunk | while | flops 402945376 | bytes 20688740 | solution.py:108
  52.9 14.0 %all_gather.30 = bf16[32,8,256]{2,0,1:T(8,128)(2,1)S(1)} all-gather(bf16[32,1,256]{2,0,1:T(8,128)(2,1)S(1)} %copy.62), channel_id=1, replica_groups=mesh['grp'=4,'row'=8] {'row'}, dimensions={1}, use_global_device_ids=true | all-gather | bytes 147456 | tf_op jit(solution)/shard_map/while/body/eval_jaxpr/all_gather | solution.py:46
  67.5 3.5 convolution_bitcast_fusion.6
  71.5 10.4 %reduce-scatter.2.cloned.1.call-done = f32[32,1,256]{2,0,1:T(8,128)} async-done(((f32[32,8,256]{2,0,1:T(8,128)}), f32[32,1,256]{2,0,1:T(8,128)}) %reduce-scatter.2.cloned.1.call-update) | async-done | bytes 32784 | tf_op jit(solution)/shard_map/while/body/eval_jaxpr/reduce_scatter | solution.py:61
  82.9 10.1 %all-gather.4 = f32[128,4,256]{2,1,0:T(4,128)S(1)} all-gather(f32[32,4,256]{2,1,0:T(4,128)S(1)} %broadcast_multiply_fusion.2), channel_id=2, replica_groups=mesh['grp'=4,'row'=8] {'grp'}, dimensions={0}, use_global_device_ids=true | all-gather | bytes 655360 | tf_op jit(solution)/shard_map/while/body/eval_jaxpr/all_gather | solution.py:75
  94.1 26.0 %all-reduce.2 = (f32[32,128]{1,0:T(8,128)S(1)}, f32[32,32]{0,1:T(8,128)S(1)}) all-reduce(f32[32,128]{1,0:T(8,128)S(1)} %fusion.102, f32[32,32]{0,1:T(8,128)S(1)} %fusion.103), channel_id=1, replica_groups=mesh['grp'=4,'row'=8] {'row'}, use_global_device_ids=true, to_apply=%region_7.9 | all-reduce | flops 5120 | bytes 40960 | tf_op jit(solution)/shard_map/while/body/eval_jaxpr/psum | solution.py:78
  131.8 3.0 convolution_bitcast_fusion.7
  136.2 14.0 %all_gather.30 = bf16[32,8,256]{2,0,1:T(8,128)(2,1)S(1)} all-gather(bf16[32,1,256]{2,0,1:T(8,128)(2,1)S(1)} %copy.62), channel_id=1, replica_groups=mesh['grp'=4,'row'=8] {'row'}, dimensions={1}, use_global_device_ids=true | all-gather | bytes 147456 | tf_op jit(solution)/shard_map/while/body/eval_jaxpr/all_gather | solution.py:46
  150.9 3.5 convolution_bitcast_fusion.6
  154.8 9.6 %reduce-scatter.2.cloned.1.call-done = f32[32,1,256]{2,0,1:T(8,128)} async-done(((f32[32,8,256]{2,0,1:T(8,128)}), f32[32,1,256]{2,0,1:T(8,128)}) %reduce-scatter.2.cloned.1.call-update) | async-done | bytes 32784 | tf_op jit(solution)/shard_map/while/body/eval_jaxpr/reduce_scatter | solution.py:61
  165.5 10.2 %all-gather.4 = f32[128,4,256]{2,1,0:T(4,128)S(1)} all-gather(f32[32,4,256]{2,1,0:T(4,128)S(1)} %broadcast_multiply_fusion.2), channel_id=2, replica_groups=mesh['grp'=4,'row'=8] {'grp'}, dimensions={0}, use_global_device_ids=true | all-gather | bytes 655360 | tf_op jit(solution)/shard_map/while/body/eval_jaxpr/all_gather | solution.py:75
  176.7 26.0 %all-reduce.2 = (f32[32,128]{1,0:T(8,128)S(1)}, f32[32,32]{0,1:T(8,128)S(1)}) all-reduce(f32[32,128]{1,0:T(8,128)S(1)} %fusion.102, f32[32,32]{0,1:T(8,128)S(1)} %fusion.103), channel_id=1, replica_groups=mesh['grp'=4,'row'=8] {'row'}, use_global_device_ids=true, to_apply=%region_7.9 | all-reduce | flops 5120 | bytes 40960 | tf_op jit(solution)/shard_map/while/body/eval_jaxpr/psum | solution.py:78
  218.8 14.0 %all_gather.30 = bf16[32,8,256]{2,0,1:T(8,128)(2,1)S(1)} all-gather(bf16[32,1,256]{2,0,1:T(8,128)(2,1)S(1)} %copy.62), channel_id=1, replica_groups=mesh['grp'=4,'row'=8] {'row'}, dimensions={1}, use_global_device_ids=true | all-gather | bytes 147456 | tf_op jit(solution)/shard_map/while/body/eval_jaxpr/all_gather | solution.py:46
  233.4 3.5 convolution_bitcast_fusion.6
  237.4 9.7 %reduce-scatter.2.cloned.1.call-done = f32[32,1,256]{2,0,1:T(8,128)} async-done(((f32[32,8,256]{2,0,1:T(8,128)}), f32[32,1,256]{2,0,1:T(8,128)}) %reduce-scatter.2.cloned.1.call-update) | async-done | bytes 32784 | tf_op jit(solution)/shard_map/while/body/eval_jaxpr/reduce_scatter | solution.py:61
  248.1 10.1 %all-gather.4 = f32[128,4,256]{2,1,0:T(4,128)S(1)} all-gather(f32[32,4,256]{2,1,0:T(4,128)S(1)} %broadcast_multiply_fusion.2), channel_id=2, replica_groups=mesh['grp'=4,'row'=8] {'grp'}, dimensions={0}, use_global_device_ids=true | all-gather | bytes 655360 | tf_op jit(solution)/shard_map/while/body/eval_jaxpr/all_gather | solution.py:75
  259.2 26.0 %all-reduce.2 = (f32[32,128]{1,0:T(8,128)S(1)}, f32[32,32]{0,1:T(8,128)S(1)}) all-reduce(f32[32,128]{1,0:T(8,128)S(1)} %fusion.102, f32[32,32]{0,1:T(8,128)S(1)} %fusion.103), channel_id=1, replica_groups=mesh['grp'=4,'row'=8] {'row'}, use_global_device_ids=true, to_apply=%region_7.9 | all-reduce | flops 5120 | bytes 40960 | tf_op jit(solution)/shard_map/while/body/eval_jaxpr/psum | solution.py:78
  296.9 3.0 convolution_bitcast_fusion.7
  301.3 14.0 %all_gather.30 = bf16[32,8,256]{2,0,1:T(8,128)(2,1)S(1)} all-gather(bf16[32,1,256]{2,0,1:T(8,128)(2,1)S(1)} %copy.62), channel_id=1, replica_groups=mesh['grp'=4,'row'=8] {'row'}, dimensions={1}, use_global_device_ids=true | all-gather | bytes 147456 | tf_op jit(solution)/shard_map/while/body/eval_jaxpr/all_gather | solution.py:46
  316.0 3.5 convolution_bitcast_fusion.6
  319.9 9.6 %reduce-scatter.2.cloned.1.call-done = f32[32,1,256]{2,0,1:T(8,128)} async-done(((f32[32,8,256]{2,0,1:T(8,128)}), f32[32,1,256]{2,0,1:T(8,128)}) %reduce-scatter.2.cloned.1.call-update) | async-done | bytes 32784 | tf_op jit(solution)/shard_map/while/body/eval_jaxpr/reduce_scatter | solution.py:61
  330.6 10.0 %all-gather.4 = f32[128,4,256]{2,1,0:T(4,128)S(1)} all-gather(f32[32,4,256]{2,1,0:T(4,128)S(1)} %broadcast_multiply_fusion.2), channel_id=2, replica_groups=mesh['grp'=4,'row'=8] {'grp'}, dimensions={0}, use_global_device_ids=true | all-gather | bytes 655360 | tf_op jit(solution)/shard_map/while/body/eval_jaxpr/all_gather | solution.py:75
  341.7 26.0 %all-reduce.2 = (f32[32,128]{1,0:T(8,128)S(1)}, f32[32,32]{0,1:T(8,128)S(1)}) all-reduce(f32[32,128]{1,0:T(8,128)S(1)} %fusion.102, f32[32,32]{0,1:T(8,128)S(1)} %fusion.103), channel_id=1, replica_groups=mesh['grp'=4,'row'=8] {'row'}, use_global_device_ids=true, to_apply=%region_7.9 | all-reduce | flops 5120 | bytes 40960 | tf_op jit(solution)/shard_map/while/body/eval_jaxpr/psum | solution.py:78
  (195 shorter events, 78.9 us)
Async XLA Ops:
  7.2 0.9 copy-start
  46.5 5.1 %copy-start.3 = (s32[32]{0:T(128)S(1)}, s32[32]{0:T(128)}, u32[]{:S(2)}) copy-start(s32[32]{0:T(128)} %get-tuple-element.491) | copy-start | bytes 388 | tf_op jit(solution)/shard_map/while
  46.5 35.4 %reduce-scatter.2.cloned.1.call-start = ((), (), s32[]{:S(2)}) async-start(), calls=%async_computation.1 | async-start | bytes 294912 | tf_op jit(solution)/shard_map/while/body/eval_jaxpr/reduce_scatter | solution.py:61
  51.5 19.5 %copy-start.4 = (s32[32]{0:T(128)S(1)}, s32[32]{0:T(128)}, u32[]{:S(2)}) copy-start(s32[32]{0:T(128)} %get-tuple-element.494) | copy-start | bytes 388 | tf_op jit(solution)/shard_map/while
  67.5 25.7 %copy-start.2 = (f32[1024]{0:T(1024)S(1)}, f32[1024]{0:T(1024)}, u32[]{:S(2)}) copy-start(f32[1024]{0:T(1024)} %get-tuple-element.495) | copy-start | bytes 12292 | tf_op jit(solution)/shard_map/while
  129.8 5.1 %copy-start.3 = (s32[32]{0:T(128)S(1)}, s32[32]{0:T(128)}, u32[]{:S(2)}) copy-start(s32[32]{0:T(128)} %get-tuple-element.491) | copy-start | bytes 388 | tf_op jit(solution)/shard_map/while
  129.8 34.6 %reduce-scatter.2.cloned.1.call-start = ((), (), s32[]{:S(2)}) async-start(), calls=%async_computation.1 | async-start | bytes 294912 | tf_op jit(solution)/shard_map/while/body/eval_jaxpr/reduce_scatter | solution.py:61
  134.9 19.5 %copy-start.4 = (s32[32]{0:T(128)S(1)}, s32[32]{0:T(128)}, u32[]{:S(2)}) copy-start(s32[32]{0:T(128)} %get-tuple-element.494) | copy-start | bytes 388 | tf_op jit(solution)/shard_map/while
  150.8 24.9 %copy-start.2 = (f32[1024]{0:T(1024)S(1)}, f32[1024]{0:T(1024)}, u32[]{:S(2)}) copy-start(f32[1024]{0:T(1024)} %get-tuple-element.495) | copy-start | bytes 12292 | tf_op jit(solution)/shard_map/while
  212.4 5.1 %copy-start.3 = (s32[32]{0:T(128)S(1)}, s32[32]{0:T(128)}, u32[]{:S(2)}) copy-start(s32[32]{0:T(128)} %get-tuple-element.491) | copy-start | bytes 388 | tf_op jit(solution)/shard_map/while
  212.4 34.6 %reduce-scatter.2.cloned.1.call-start = ((), (), s32[]{:S(2)}) async-start(), calls=%async_computation.1 | async-start | bytes 294912 | tf_op jit(solution)/shard_map/while/body/eval_jaxpr/reduce_scatter | solution.py:61
  217.5 19.5 %copy-start.4 = (s32[32]{0:T(128)S(1)}, s32[32]{0:T(128)}, u32[]{:S(2)}) copy-start(s32[32]{0:T(128)} %get-tuple-element.494) | copy-start | bytes 388 | tf_op jit(solution)/shard_map/while
  233.4 24.9 %copy-start.2 = (f32[1024]{0:T(1024)S(1)}, f32[1024]{0:T(1024)}, u32[]{:S(2)}) copy-start(f32[1024]{0:T(1024)} %get-tuple-element.495) | copy-start | bytes 12292 | tf_op jit(solution)/shard_map/while
  294.9 5.1 %copy-start.3 = (s32[32]{0:T(128)S(1)}, s32[32]{0:T(128)}, u32[]{:S(2)}) copy-start(s32[32]{0:T(128)} %get-tuple-element.491) | copy-start | bytes 388 | tf_op jit(solution)/shard_map/while
  294.9 34.6 %reduce-scatter.2.cloned.1.call-start = ((), (), s32[]{:S(2)}) async-start(), calls=%async_computation.1 | async-start | bytes 294912 | tf_op jit(solution)/shard_map/while/body/eval_jaxpr/reduce_scatter | solution.py:61
  300.0 19.5 %copy-start.4 = (s32[32]{0:T(128)S(1)}, s32[32]{0:T(128)}, u32[]{:S(2)}) copy-start(s32[32]{0:T(128)} %get-tuple-element.494) | copy-start | bytes 388 | tf_op jit(solution)/shard_map/while
  315.9 24.8 %copy-start.2 = (f32[1024]{0:T(1024)S(1)}, f32[1024]{0:T(1024)}, u32[]{:S(2)}) copy-start(f32[1024]{0:T(1024)} %get-tuple-element.495) | copy-start | bytes 12292 | tf_op jit(solution)/shard_map/while
  377.4 0.7 copy-start.1
Sparse Core Ops, SparseCore 0:
  52.9 28.9 reduce-scatter.1
  136.2 28.1 reduce-scatter.1
  218.8 28.2 reduce-scatter.1
  301.3 28.1 reduce-scatter.1
